TPU v7x, 32 devices: a whole 2x2x4 slice. The times are simulated.
32 devices in a mesh: blk: 8 (over z, x), grp: 4 (over y, core).
Axes of the slice: x: 2, y: 2, z: 4, core: 2. Of those that a mesh axis runs over, the one named last changes fastest.
Arguments:
- coil_pos: float32 [3, 1280], P(None, ('blk', 'grp')), may hold values from -1 to 1
- coil_radius: float32 [1280], P(('blk', 'grp')), may hold values from 0.02 to 0.08
- coil_current: bfloat16 [64, 1280], P(None, ('blk', 'grp')), may hold values from -0.3125 to 0.3125
- blank_pos: float32 [3, 4096], P(None, ('blk', 'grp')), may hold values from -1 to 1
- blank_rule: int32 [4096], P(('blk', 'grp')), may hold values from 0 to 7
- blank_cond: float32 [4096], P(('blk', 'grp')), may hold values from 0.3 to 3
- quad_offset: float32 [3, 8, 2], replicated, may hold values from -0.1 to 0.1
- quad_weight: float32 [8, 2], replicated, may hold values from 0.3 to 0.7
Outputs:
- blank_current: bfloat16 [64, 4096], P(None, ('blk', 'grp'))
- coil_reaction: float32 [64, 1280], P(None, ('blk', 'grp'))
All inputs are finite; a program needn't handle non-finite values.
Results may differ from a plain program's by a relative error of at most 0.0066.
Values may be sent and summed in bfloat16 or wider, within the bound.
A program may use at most 64 MiB of HBM per device.

v0:
```python
import math

import jax
import jax.numpy as jnp
from jax import lax
from jax.sharding import PartitionSpec as P


def blank_geometry(blank_pos, blank_rule, quad_offset, quad_weight):
    rules = quad_weight.shape[0]
    points = quad_weight.shape[1]
    onehot = (blank_rule[None, :] == jnp.arange(rules, dtype=jnp.int32)[:, None]).astype(
        jnp.float32
    )
    table_rows = []
    base_rows = []
    zeros_row = jnp.zeros_like(blank_pos[0])
    for point in range(points):
        table_rows += [
            quad_offset[0, :, point],
            quad_offset[1, :, point],
            quad_offset[2, :, point],
            quad_weight[:, point],
        ]
        base_rows += [blank_pos[0], blank_pos[1], blank_pos[2], zeros_row]
    table = jnp.stack(table_rows, 0)
    base = jnp.stack(base_rows, 0)
    return base + jnp.dot(table, onehot, precision=lax.Precision.HIGHEST)


def kernel_block(coil_geometry, geometry):
    points = geometry.shape[0] // 4
    running = jnp.zeros((coil_geometry.shape[1], geometry.shape[1]), jnp.float32)
    for point in range(points):
        delta_x = coil_geometry[0][:, None] - geometry[4 * point][None, :]
        delta_y = coil_geometry[1][:, None] - geometry[4 * point + 1][None, :]
        delta_z = coil_geometry[2][:, None] - geometry[4 * point + 2][None, :]
        squared = (
            delta_x * delta_x + delta_y * delta_y + delta_z * delta_z + coil_geometry[3][:, None]
        )
        running = running + geometry[4 * point + 3][None, :] * lax.rsqrt(squared)
    return running


def blockwise(width, limit, step_fn, initial):
    block = math.gcd(width, limit)
    count = width // block

    def advance(index, carried):
        start = (index * block).astype(jnp.int32)
        return step_fn(carried, start, block)

    return lax.fori_loop(0, count, advance, initial)


def per_device(
    coil_pos, coil_radius, coil_current, blank_pos, blank_rule, blank_cond, quad_offset, quad_weight
):
    coil_geometry = jnp.concatenate([coil_pos, (coil_radius * coil_radius)[None, :]], 0)
    geometry = blank_geometry(blank_pos, blank_rule, quad_offset, quad_weight)
    samples = coil_current.shape[0]
    coil_count = coil_current.shape[1]
    local_blanks = geometry.shape[1]
    total_blanks = local_blanks * lax.axis_size("blk") * lax.axis_size("grp")
    all_current = lax.all_gather(coil_current, ("blk", "grp"), axis=1, tiled=True)
    portion = lax.all_gather(coil_geometry, ("blk", "grp"), axis=1, tiled=True)

    def collect_inner(carried, start, block):
        rows = lax.dynamic_slice_in_dim(portion, start, block, 1)
        kernel_tile = kernel_block(rows, geometry).astype(jnp.bfloat16)
        currents = lax.dynamic_slice_in_dim(all_current, start, block, 1)
        return carried + jnp.dot(currents, kernel_tile, preferred_element_type=jnp.float32)

    induced = blockwise(
        portion.shape[1], 2048, collect_inner, jnp.zeros((samples, local_blanks), jnp.float32)
    )
    blank_current = induced.astype(jnp.bfloat16)
    weighted = (blank_cond[None, :] * blank_current.astype(jnp.float32)).astype(jnp.bfloat16)
    all_weighted = lax.all_gather(weighted, ("blk", "grp"), axis=1, tiled=True)
    reflect_portion = lax.all_gather(geometry, ("blk", "grp"), axis=1, tiled=True)

    def reflect_inner(carried, start, block):
        columns = lax.dynamic_slice_in_dim(reflect_portion, start, block, 1)
        kernel_tile = kernel_block(coil_geometry, columns).astype(jnp.bfloat16)
        currents = lax.dynamic_slice_in_dim(all_weighted, start, block, 1)
        return carried + lax.dot_general(
            currents, kernel_tile, (((1,), (1,)), ((), ())), preferred_element_type=jnp.float32
        )

    reaction = blockwise(
        reflect_portion.shape[1], 2048, reflect_inner, jnp.zeros((samples, coil_count), jnp.float32)
    )
    coil_reaction = reaction * (2.0 / total_blanks)
    return (blank_current, coil_reaction)


def solution(mesh):
    in_specs = (
        P(None, ("blk", "grp")),
        P(("blk", "grp")),
        P(None, ("blk", "grp")),
        P(None, ("blk", "grp")),
        P(("blk", "grp")),
        P(("blk", "grp")),
        P(),
        P(),
    )
    out_specs = (P(None, ("blk", "grp")), P(None, ("blk", "grp")))
    return jax.shard_map(
        per_device, mesh=mesh, in_specs=in_specs, out_specs=out_specs, check_vma=False
    )
```

profile of v0, /device:TPU:1, one launch (start us, length us, event | category | flops | bytes accessed | tf_op | source)
XLA Modules:
  0.0 166.5 jit_solution(2309037192950104632)
XLA Ops:
  0.6 0.0 copy-start.7
  0.6 0.6 copy-done.7
  1.3 0.0 copy-start.4
  1.3 0.7 copy-done.4
  2.0 0.0 copy-start
  2.0 0.0 copy-start.2
  2.0 0.7 copy-done
  2.7 0.0 copy-done.2
  2.7 0.0 copy-start.3
  2.7 0.0 copy-start.6
  2.7 0.6 copy-done.3
  3.4 0.0 copy-done.6
  3.4 0.1 convolution_add_fusion.2
  3.5 43.3 %all-gather = f32[32,40,4]{1,2,0:T(4,128)S(1)} all-gather(f32[1,40,4]{1,2,0:T(4,128)S(1)} %maximum_bitcast_fusion), channel_id=1, replica_groups=mesh['blk'=8,'grp'=4] {'blk','grp'}, dimensions={0}, use_global_device_ids=true | all-gather | bytes 21120 | tf_op jit(solution)/shard_map/all_gather | solution.py:66
  46.8 0.1 reshape.15
  46.9 0.0 copy-start.1
  46.9 37.0 %all_gather.15 = f32[8,4096]{1,0:T(8,128)S(1)} all-gather(f32[8,128]{1,0:T(8,128)S(1)} %convolution_add_fusion.2), channel_id=1, replica_groups=mesh['blk'=8,'grp'=4] {'blk','grp'}, dimensions={1}, use_global_device_ids=true | all-gather | bytes 135168 | tf_op jit(solution)/shard_map/all_gather | solution.py:80
  83.9 0.0 copy-done.1
  83.9 38.8 %all_gather.12 = bf16[64,1280]{0,1:T(8,128)(2,1)S(1)} all-gather(bf16[64,40]{0,1:T(8,128)(2,1)S(1)} %copy-done.1), channel_id=1, replica_groups=mesh['blk'=8,'grp'=4] {'blk','grp'}, dimensions={1}, use_global_device_ids=true | all-gather | bytes 168960 | tf_op jit(solution)/shard_map/all_gather | solution.py:65
  122.7 0.2 copy.14
  122.9 2.3 %while.28 = (s32[]{:T(128)}, f32[64,128]{1,0:T(8,128)S(1)}, bf16[64,1280]{1,0:T(8,128)(2,1)S(1)}, f32[8,128]{1,0:T(8,128)S(1)}, f32[4,1280]{1,0:T(4,128)S(1)}, /...) while((s32[]{:T(128)}, f32[64,128]{1,0:T(8,128)S(1)}, ...), condition=%wide.region_1.0_spmd.clone, body=%wide.region_0.0_spmd.clone.sunk | while | flops 4931594 | bytes 123117 | solution.py:53
  122.9 0.1 constant_dynamic-slice_fusion.3
  123.0 0.3 convolution_add_fusion.5
  123.4 0.1 constant_dynamic-slice_fusion.3
  123.5 0.3 convolution_add_fusion.5
  123.8 0.1 constant_dynamic-slice_fusion.3
  123.9 0.3 convolution_add_fusion.5
  124.3 0.1 constant_dynamic-slice_fusion.3
  124.4 0.3 convolution_add_fusion.5
  124.8 0.1 constant_dynamic-slice_fusion.3
  124.9 0.3 convolution_add_fusion.5
  125.2 0.0 copy-start.5
  125.2 0.6 copy-done.5
  125.9 0.6 multiply_convert_fusion
  126.5 38.0 %all_gather.14 = bf16[64,4096]{1,0:T(8,128)(2,1)S(1)} all-gather(bf16[64,128]{1,0:T(8,128)(2,1)S(1)} %get-tuple-element.278), channel_id=1, replica_groups=mesh['blk'=8,'grp'=4] {'blk','grp'}, dimensions={1}, use_global_device_ids=true | all-gather | bytes 540672 | tf_op jit(solution)/shard_map/all_gather | solution.py:79
  164.5 1.4 while.29
  164.5 0.2 fusion.36
  164.7 0.5 convolution_add_fusion.6
  165.2 0.2 fusion.36
  165.4 0.5 convolution_add_fusion.6
  165.9 0.6 broadcast_multiply_fusion
  (16 shorter events, 0.1 us)
Async XLA Ops:
  0.6 0.7 copy-start.7
  1.3 0.7 copy-start.4
  2.0 0.7 copy-start
  2.0 0.7 copy-start.2
  2.7 0.7 copy-start.3
  2.7 0.7 copy-start.6
  46.9 37.0 %copy-start.1 = (bf16[64,40]{0,1:T(8,128)(2,1)S(1)}, bf16[64,40]{0,1:T(8,128)(2,1)}, u32[]{:S(2)}) copy-start(bf16[64,40]{0,1:T(8,128)(2,1)} %param.14) | copy-start | bytes 15364
  125.2 0.7 copy-start.5
where the time goes:
time: 167 us
  blocking collectives  157 us (94%)
  local copies, waits for them, and re-layouts  4.48 us (3%)
  matrix products  2.78 us (2%)
    all_gather x1, blocking collectives, per_device(): portion = lax.all_gather(coil_geometry, ('blk', 'grp'), axis=1, tiled=True)  43.3 us
    all_gather x1, blocking collectives, per_device(): lax.all_gather(coil_current, ('blk', 'grp'), axis=1, tiled=True)  38.8 us
    all_gather x1, blocking collectives, per_device(): all_weighted = lax.all_gather(weighted, ('blk', 'grp'), axis=1, tiled=True)  38 us
    all_gather x1, blocking collectives, per_device(): lax.all_gather(geometry, ('blk', 'grp'), axis=1, tiled=True)  37 us
    unnamed x18, local copies, waits for them, and re-layouts  3.58 us

commit v1 on v0

v1 whole, which is shorter than its diff:
```python
import functools

import jax
import jax.numpy as jnp
from jax import lax
from jax.experimental import pallas as pl
from jax.experimental.pallas import tpu as pltpu
from jax.sharding import PartitionSpec as P

MESH = pl.DeviceIdType.MESH
LANES = 128


def split3(value):
    first = value.astype(jnp.bfloat16).astype(jnp.float32)
    rest = value - first
    second = rest.astype(jnp.bfloat16).astype(jnp.float32)
    third = (rest - second).astype(jnp.bfloat16).astype(jnp.float32)
    return first, second, third


def kernel(
    blks, pairs, offsets, scale,
    cpos, crad, ccur, bpos, brule, bcond, qoff, qw,
    blank_out, react_out,
    held, geo, gmat, kern, part, outgo, income, flip,
    send_sem, recv_sem, geo_send, geo_recv, part_send, part_recv, rsend_sem, rrecv_sem,
):
    samples, coils = ccur.shape
    blanks = bpos.shape[1]
    rules, points = qw.shape
    n = blks * pairs
    stride = held.shape[0] // n
    blk = lax.axis_index("blk")
    grp = lax.axis_index("grp")
    core = lax.rem(grp, 2)
    pair = lax.div(grp, 2)
    sibling = (blk, pair * 2 + 1 - core)

    def peer(index, sign):
        db, dp = offsets[index]
        if sign < 0:
            db, dp = (blks - db) % blks, (pairs - dp) % pairs
        return (lax.rem(blk + db, blks), lax.rem(pair + dp, pairs) * 2 + core)

    barrier = pltpu.get_barrier_semaphore()
    for k in range(n - 1, 0, -1):
        pl.semaphore_signal(barrier, inc=1, device_id=peer(k, 1), device_id_type=MESH)
    pl.semaphore_signal(barrier, inc=1, device_id=sibling, device_id_type=MESH)

    flip[...] = jnp.zeros_like(flip)
    flip[0:samples, 0:coils] = ccur[...].astype(jnp.float32)
    radius = crad[...].reshape(1, coils)
    xyz = [cpos[c : c + 1, :] for c in range(3)]
    fixed = xyz[0] * xyz[0] + xyz[1] * xyz[1] + xyz[2] * xyz[2] + radius * radius
    ones = jnp.ones((1, coils), jnp.float32)
    rows = []
    for c in range(3):
        a, b, d = split3(xyz[c])
        rows += [a, a, a, b, b, d]
    rows += list(split3(fixed)) + [ones, ones, ones]
    for f, row in enumerate(rows):
        flip[samples + f : samples + f + 1, 0:coils] = row
    flip[samples + 18 : samples + 19, coils:LANES] = jnp.ones((1, LANES - coils), jnp.float32)
    turned = jnp.transpose(flip[...])[0:stride].astype(jnp.bfloat16)
    held[0:stride, :] = turned
    if stride > coils:
        for k in range(1, n):
            held[k * stride + coils : (k + 1) * stride, :] = turned[coils:stride]

    onehot = (
        brule[...].reshape(1, blanks) == lax.broadcasted_iota(jnp.int32, (rules, blanks), 0)
    ).astype(jnp.float32)
    geo[0] = jnp.zeros(geo.shape[1:], jnp.float32)
    for q in range(points):
        for c in range(3):
            geo[0, 4 * q + c : 4 * q + c + 1, :] = bpos[c : c + 1, :] + jnp.sum(
                onehot * qoff[c][:, q : q + 1], axis=0, keepdims=True
            )
        geo[0, 4 * q + 3 : 4 * q + 4, :] = jnp.sum(
            onehot * qw[:, q : q + 1], axis=0, keepdims=True
        )
    geo[0, 4 * points : 4 * points + 1, :] = bcond[...].reshape(1, blanks)

    pl.semaphore_wait(barrier, n)

    copies = [None] * n
    for k in range(n - 1, 0, -1):
        copies[k] = pltpu.make_async_remote_copy(
            src_ref=held.at[pl.ds(0, coils)],
            dst_ref=held.at[pl.ds(k * stride, coils)],
            send_sem=send_sem.at[k],
            recv_sem=recv_sem.at[k],
            device_id=peer(k, 1),
            device_id_type=MESH,
        )
        copies[k].start()
    geo_copy = pltpu.make_async_remote_copy(
        src_ref=geo.at[0], dst_ref=geo.at[1], send_sem=geo_send, recv_sem=geo_recv,
        device_id=sibling, device_id_type=MESH,
    )
    geo_copy.start()
    geo_copy.wait()

    def wide(row):
        return jnp.concatenate([geo[0, row : row + 1, :], geo[1, row : row + 1, :]], axis=1)

    width = 2 * blanks
    gmat[...] = jnp.zeros_like(gmat)
    feature_block = []
    for q in range(points):
        pos = [wide(4 * q + c) for c in range(3)]
        square = pos[0] * pos[0] + pos[1] * pos[1] + pos[2] * pos[2]
        one = jnp.ones((1, width), jnp.float32)
        rows = []
        for c in range(3):
            a, b, d = (-2.0 * v for v in split3(pos[c]))
            rows += [a, b, d, a, b, a]
        rows += [one, one, one] + list(split3(square))
        feature_block.append(jnp.concatenate(rows, axis=0))
    gmat[samples : samples + len(rows), :] = jnp.concatenate(feature_block, axis=1).astype(
        jnp.bfloat16
    )
    weights = [wide(4 * q + 3) for q in range(points)]
    cond = wide(4 * points)

    group = 4 if n % 4 == 0 else 1
    total = jnp.zeros((LANES, width), jnp.float32)
    for first in range(0, n, group):
        for k in range(first, first + group):
            if k > 0:
                copies[k].wait_recv()
        block = held[first * stride : (first + group) * stride, :]
        squared = jnp.dot(block, gmat[...], preferred_element_type=jnp.float32)
        tile = weights[0] * lax.rsqrt(squared[:, 0:width])
        for q in range(1, points):
            tile = tile + weights[q] * lax.rsqrt(squared[:, q * width : (q + 1) * width])
        tile = tile.astype(jnp.bfloat16)
        kern[first * stride : (first + group) * stride, :] = tile
        total = total + lax.dot_general(
            block, tile, (((0,), (0,)), ((), ())), preferred_element_type=jnp.float32
        )
    part[0] = total[0:samples]
    part_copy = pltpu.make_async_remote_copy(
        src_ref=part.at[0], dst_ref=part.at[1], send_sem=part_send, recv_sem=part_recv,
        device_id=sibling, device_id_type=MESH,
    )
    part_copy.start()
    part_copy.wait_recv()
    other = jnp.concatenate([part[1, :, blanks:width], part[1, :, 0:blanks]], axis=1)
    induced = (total[0:samples] + other).astype(jnp.bfloat16)
    blank_out[...] = induced[:, 0:blanks]
    weighted = (cond * induced.astype(jnp.float32)).astype(jnp.bfloat16)
    weighted = jnp.concatenate(
        [weighted, jnp.zeros((LANES - samples, width), jnp.bfloat16)], axis=0
    )

    returns = [None] * n
    own = None
    for first in range(n - group, -1, -group):
        product = lax.dot_general(
            kern[first * stride : (first + group) * stride, :],
            weighted,
            (((1,), (1,)), ((), ())),
            preferred_element_type=jnp.float32,
        )
        if first == 0:
            own = product[0:coils]
        outgo[first * stride : (first + group) * stride, :] = product.astype(jnp.bfloat16)
        for k in range(first + group - 1, first - 1, -1):
            if k > 0:
                returns[k] = pltpu.make_async_remote_copy(
                    src_ref=outgo.at[pl.ds(k * stride, coils)],
                    dst_ref=income.at[pl.ds(k * stride, coils)],
                    send_sem=rsend_sem.at[k],
                    recv_sem=rrecv_sem.at[k],
                    device_id=peer(k, -1),
                    device_id_type=MESH,
                )
                returns[k].start()

    flip[...] = jnp.zeros_like(flip)
    for k in range(1, n):
        copies[k].wait_send()
    part_copy.wait_send()
    for k in range(1, n):
        returns[k].wait_recv()
        own = own + income[k * stride : k * stride + coils, :].astype(jnp.float32)
    flip[0:coils, :] = own * scale
    react_out[...] = jnp.transpose(flip[...])[0:samples, 0:coils]
    for k in range(1, n):
        returns[k].wait_send()


def per_device(
    blks, grps,
    coil_pos, coil_radius, coil_current, blank_pos, blank_rule, blank_cond, quad_offset, quad_weight,
):
    pairs = grps // 2
    n = blks * pairs
    samples, coils = coil_current.shape
    blanks = blank_pos.shape[1]
    points = quad_weight.shape[1]
    stride = -(-coils // 16) * 16
    offsets = sorted(
        ((b, p) for b in range(blks) for p in range(pairs)),
        key=lambda o: min(o[0], blks - o[0]) + min(o[1], pairs - o[1]),
    )
    scale = 2.0 / (blanks * blks * grps)
    vmem = pl.BlockSpec(memory_space=pltpu.VMEM)
    return pl.pallas_call(
        functools.partial(kernel, blks, pairs, tuple(offsets), scale),
        out_shape=(
            jax.ShapeDtypeStruct((samples, blanks), jnp.bfloat16),
            jax.ShapeDtypeStruct((samples, coils), jnp.float32),
        ),
        in_specs=[vmem] * 8,
        out_specs=(vmem, vmem),
        scratch_shapes=[
            pltpu.VMEM((n * stride, LANES), jnp.bfloat16),
            pltpu.VMEM((2, -(-(4 * points + 1) // 8) * 8, blanks), jnp.float32),
            pltpu.VMEM((LANES, points * 2 * blanks), jnp.bfloat16),
            pltpu.VMEM((n * stride, 2 * blanks), jnp.bfloat16),
            pltpu.VMEM((2, samples, 2 * blanks), jnp.float32),
            pltpu.VMEM((n * stride, LANES), jnp.bfloat16),
            pltpu.VMEM((n * stride, LANES), jnp.bfloat16),
            pltpu.VMEM((LANES, LANES), jnp.float32),
            pltpu.SemaphoreType.DMA((n,)),
            pltpu.SemaphoreType.DMA((n,)),
            pltpu.SemaphoreType.DMA,
            pltpu.SemaphoreType.DMA,
            pltpu.SemaphoreType.DMA,
            pltpu.SemaphoreType.DMA,
            pltpu.SemaphoreType.DMA((n,)),
            pltpu.SemaphoreType.DMA((n,)),
        ],
        compiler_params=pltpu.CompilerParams(collective_id=0, has_side_effects=True),
    )(
        coil_pos, coil_radius, coil_current, blank_pos, blank_rule, blank_cond,
        quad_offset, quad_weight,
    )


def solution(mesh):
    split = ("blk", "grp")
    in_specs = (
        P(None, split), P(split), P(None, split), P(None, split), P(split), P(split), P(), P(),
    )
    return jax.shard_map(
        functools.partial(per_device, mesh.shape["blk"], mesh.shape["grp"]),
        mesh=mesh,
        in_specs=in_specs,
        out_specs=(P(None, split), P(None, split)),
        check_vma=False,
    )
```

time: 167 us -> 27.9 us (0.17)
  blocking collectives: 157 us -> 0 us
  Pallas kernels: 0 us -> 22 us
  matrix products: 2.78 us -> 0 us
    all_gather x4 -> x0, blocking collectives: 157 us -> none  [the longest x1 43.3 us: per_device(): portion = lax.all_gather(coil_geometry, ('blk', 'grp'), axis=1, tiled=True)]
    pallas_call x0 -> x1, Pallas kernels: none -> 22 us  [per_device(): pl.pallas_call(functools.partial(kernel, blks, pairs, tuple(offsets), sca...]
    dot_general x8 -> x0, matrix products: 2.78 us -> none  [the longest x5 1.7 us: collect_inner(): jnp.dot(currents, kernel_tile, preferred_element_type=jnp.float32)]
    unnamed x18 -> x10, local copies, waits for them, and re-layouts: 3.58 us -> 3.36 us
where the time goes in v1:
time: 27.9 us; the launch traced here: 27.4 us
  Pallas kernels  22 us (79%)
  local copies, waits for them, and re-layouts  4.81 us (17%)
  between operations  0.67 us (2%)
    pallas_call x1, Pallas kernels, per_device(): pl.pallas_call(functools.partial(kernel, blks, pairs, tuple(offsets), sca...  22 us
    unnamed x10, local copies, waits for them, and re-layouts  3.36 us
    pallas_call x1, local copies, waits for them, and re-layouts, per_device(): pl.pallas_call(functools.partial(kernel, blks, pairs, tuple(offsets), sca...  1.45 us

profile of v1, /device:TPU:1, one launch (start us, length us, event | category | flops | bytes accessed | tf_op | source)
XLA Modules:
  0.0 27.4 jit_solution(8887348902016347325)
XLA Ops:
  0.6 0.0 copy-start.2
  0.6 0.0 copy-start.1
  0.7 1.4 %copy.12.qw = f32[8,2]{1,0:T(8,128)} copy(f32[8,2]{0,1:T(2,128)} %param.15) | data formatting | bytes 128 | tf_op args[7]
  2.0 0.0 copy-done.2
  2.0 0.7 %copy.11.qoff = f32[3,8,2]{2,1,0:T(8,128)} copy(f32[3,8,2]{1,2,0:T(2,128)S(1)} %copy-done.2) | data formatting | bytes 384 | tf_op args[6]
  2.7 0.0 copy-done.1
  2.7 0.7 %copy.10.ccur = bf16[64,40]{1,0:T(8,128)(2,1)} copy(bf16[64,40]{0,1:T(8,128)(2,1)S(1)} %copy-done.1) | data formatting | bytes 10240 | tf_op args[2]
  3.4 22.0 %shard_map.95 = (bf16[64,128]{1,0:T(8,128)(2,1)}, f32[64,40]{1,0:T(8,128)}) custom-call(f32[3,40]{1,0:T(4,128)} %cpos.1, f32[40]{0:T(128)} %crad.1, bf16[64,40]{1,0:T(8,128)(2,1)} %copy.10.ccur, f32[3,128]{1,0:T(4,128)} %bpos.1, s32[128]{0:T(128)} %brule.1, f32[128]{0:T(128)} %bcond.1, f32[3,8,2]{2,1,0:T(8,128)} %copy.11.qoff, f32[8,2]{1,0:T(8,128)} %copy.12.qw), custom_call_target="tpu_custom_call" | custom-call | tf_op jit(solution)/shard_map/pallas_call | solution.py:211
  25.4 0.0 copy-start
  25.4 1.4 %copy.13 = f32[64,40]{0,1:T(8,128)} copy(f32[64,40]{1,0:T(8,128)} %get-tuple-element.3) | data formatting | bytes 20480 | tf_op jit(solution)/shard_map/pallas_call | solution.py:211
  26.8 0.0 copy-done
  26.8 0.6 %copy.15 = bf16[64,128]{1,0:T(8,128)(2,1)} copy(bf16[64,128]{1,0:T(8,128)(2,1)S(1)} %copy-done) | data formatting | bytes 32768
Async XLA Ops:
  0.6 1.4 %copy-start.2 = (f32[3,8,2]{1,2,0:T(2,128)S(1)}, f32[3,8,2]{1,2,0:T(2,128)}, u32[]{:S(2)}) copy-start(f32[3,8,2]{1,2,0:T(2,128)} %param.14) | copy-start | bytes 580
  0.6 2.1 %copy-start.1 = (bf16[64,40]{0,1:T(8,128)(2,1)S(1)}, bf16[64,40]{0,1:T(8,128)(2,1)}, u32[]{:S(2)}) copy-start(bf16[64,40]{0,1:T(8,128)(2,1)} %param.10) | copy-start | bytes 15364
  25.4 1.5 %copy-start = (bf16[64,128]{1,0:T(8,128)(2,1)S(1)}, bf16[64,128]{1,0:T(8,128)(2,1)}, u32[]{:S(2)}) copy-start(bf16[64,128]{1,0:T(8,128)(2,1)} %get-tuple-element.6) | copy-start | bytes 49156
